TPU v7x, 32 devices: a whole 2x2x4 slice. The times are simulated.
32 devices in a mesh: dom: 4 (over y, core), rep: 8 (over z, x).
Axes of the slice: x: 2, y: 2, z: 4, core: 2. Of those that a mesh axis runs over, the one named last changes fastest.
Arguments:
- facts: float32 [131072, 256], P(('dom', 'rep')), may hold values from -6 to 6
- row_owner: int32 [131072, 1], P(('dom', 'rep')), may hold values from 0 to 3; in each aligned block of 4096 rows (0 to 4095, 4096 to 8191, ...) at most 2048 rows name the same one
- key_offset: int32 [131072], P(('dom', 'rep')), may hold values from 0 to 1023
Outputs:
- key_means: float32 [4096, 256], P(('dom', 'rep'))
- key_counts: float32 [4096], P(('dom', 'rep'))
Inputs may be any that keep to these rules, and one draw needn't show every extreme that they name: `row_owner`: in the rows of one device no key range is named by more than 2048 rows, a bound that some block reaches.
All inputs are finite; a program needn't handle non-finite values.
Results may differ from a plain program's by a relative error of at most 0.0003.
Values sent between devices are 32-bit elements; how exact they have to be, the bound alone decides.
A program may use at most 64 MiB of HBM per device.

v0:
```python
import functools

import jax
import jax.numpy as jnp
from jax import lax
from jax.experimental import pallas as pl
from jax.experimental.pallas import tpu as pltpu
from jax.sharding import PartitionSpec as P

KEYS = 4096
MESH = pl.DeviceIdType.MESH
F32 = jnp.float32
BF16 = jnp.bfloat16


def flip(index, bits):
    at = 1
    while at <= bits:
        if bits & at:
            index = index + at * (1 - 2 * ((index // at) % 2))
        at *= 2
    return index


def kernel(D, Z, hb, rows, M, chunk, owner_hbm, offset_hbm, facts_ref, out_ref, cout_ref,
           owner_ref, offset_ref, lab_ref, fbuf, high, low, tab, recvC1, recvC2,
           rA1, rB1, rA2, rB2, rZ,
           c0, cS, cR, cD, cX, cXr, cZ, cZr, fsem, isem,
           sC1, tC1, sC2, tC2, sA1, tA1, sB1, tB1, sA2, tA2, sB2, tB2, sZ, tZ,
           scC, tcC, scD, tcD, scX, tcX, scZ, tcZ):
    me_d, me_r = lax.axis_index("dom"), lax.axis_index("rep")
    T1, T2 = (3 * D - 2) * hb, (D + 2) * hb
    stage = 4 * D * hb
    core = (flip(me_d, 1), me_r)
    dpeer = [None] + [(flip(me_d, 2 * d), me_r) for d in range(1, D)]
    xpeer = (me_d, flip(me_r, 1))
    zpeer = [None] + [(me_d, flip(me_r, 2 * z)) for z in range(1, Z)]
    peers = [core] + dpeer[1:] + [xpeer] + zpeer[1:]

    nchunks = rows // chunk
    loads = [
        pltpu.make_async_copy(
            facts_ref.at[pl.ds(k * chunk, chunk)], fbuf.at[pl.ds(k * chunk, chunk)], fsem.at[k]
        )
        for k in range(nchunks)
    ]
    ints = [
        pltpu.make_async_copy(owner_hbm, owner_ref, isem.at[0]),
        pltpu.make_async_copy(offset_hbm, offset_ref, isem.at[1]),
    ]
    for ld in ints + loads:
        ld.start()
    barrier = pltpu.get_barrier_semaphore()
    for p in peers:
        pl.semaphore_signal(barrier, inc=1, device_id=p, device_id_type=MESH)

    def rcopy(src, dst, s, t, dev):
        return pltpu.make_async_remote_copy(
            src_ref=src, dst_ref=dst, send_sem=s, recv_sem=t, device_id=dev, device_id_type=MESH
        )

    nrow = 4 * D * Z
    kpd = 2 * hb
    for ld in ints:
        ld.wait()
    rel = owner_ref[...] ^ me_d
    dc, d = rel & 1, rel >> 1
    offset = offset_ref[...]
    i = offset & (kpd - 1)
    rr = (offset >> (kpd.bit_length() - 1)) ^ me_r
    x, z = rr & 1, rr >> 1
    ii = i & (hb - 1)
    blk_a = jnp.where(d > 0, 2 * (d - 1) + x, jnp.where(x > 0, 3 * D - 2, 4 * D - 2))
    blk_b = jnp.where(x > 0, 2 * (D - 1) + d, jnp.where(d > 0, 3 * D - 2 + d, 4 * D - 1))
    blk = jnp.where(i >= hb, blk_b, blk_a)
    lab_ref[...] = (((Z - 1 - z) * 2 + dc) * (4 * D) + blk) * hb + ii
    crow = ((dc * D + d) * 2 + x) * Z + z
    hot_r = jnp.where(lax.broadcasted_iota(jnp.int32, (nrow, rows), 0) == crow, 1.0, 0.0).astype(BF16)
    hot_c = jnp.where(lax.broadcasted_iota(jnp.int32, (kpd, rows), 0) == i, 1.0, 0.0).astype(BF16)
    cnt = lax.dot_general(hot_r, hot_c, (((1,), (1,)), ((), ())), preferred_element_type=F32)
    half = nrow // 2
    for d in range(D):
        c0[d] = cnt[d * 2 * Z:(d + 1) * 2 * Z]
        cS[d] = cnt[half + d * 2 * Z:half + (d + 1) * 2 * Z]

    for k in range(nchunks):
        loads[k].wait()

        @pl.loop(0, chunk // 256)
        def _(j):
            at = pl.multiple_of(k * chunk + j * 256, 256)
            v = fbuf[pl.ds(at, 256), :]
            hi = v.astype(BF16)
            high[pl.ds(at, 256), :] = hi
            low[pl.ds(at, 256), :] = (v - hi.astype(F32)).astype(BF16)

    pl.semaphore_wait(barrier, len(peers))
    cc = rcopy(cS, cR, scC, tcC, core)
    cc.start()

    def tile(start, size):
        rel = lab_ref[...] - start
        total = None
        for k in range(nchunks):
            part = rel[:, k * chunk:(k + 1) * chunk]
            hot = jnp.where(lax.broadcasted_iota(jnp.int32, (size, chunk), 0) == part, 1.0, 0.0).astype(BF16)
            at = slice(k * chunk, (k + 1) * chunk)
            o = jnp.dot(hot, high[at, :], preferred_element_type=F32) + jnp.dot(
                hot, low[at, :], preferred_element_type=F32
            )
            total = o if total is None else total + o
        return total

    def C1(i):
        return rcopy(tab.at[4 * i, pl.ds(0, T1)], recvC1.at[i], sC1.at[i], tC1.at[i], core)

    def C2(i):
        return rcopy(tab.at[4 * i + 2, pl.ds(0, T2)], recvC2.at[i], sC2.at[i], tC2.at[i], core)

    def A1(i, d):
        return rcopy(tab.at[4 * i + 1, pl.ds(2 * (d - 1) * hb, 2 * hb)], rA1.at[i, d - 1],
                     sA1.at[i, d - 1], tA1.at[i, d - 1], dpeer[d])

    def B1(i):
        return rcopy(tab.at[4 * i + 1, pl.ds(2 * (D - 1) * hb, D * hb)], rB1.at[i], sB1.at[i], tB1.at[i], xpeer)

    def A2(i):
        return rcopy(tab.at[4 * i + 3, pl.ds(0, hb)], rA2.at[i], sA2.at[i], tA2.at[i], xpeer)

    def B2(i, d):
        return rcopy(tab.at[4 * i + 3, pl.ds(d * hb, hb)], rB2.at[i, d - 1], sB2.at[i, d - 1], tB2.at[i, d - 1], dpeer[d])

    def ZC(i, z):
        return rcopy(tab.at[4 * i + 3, pl.ds(D * hb, 2 * hb)], rZ.at[i], sZ.at[i], tZ.at[i], zpeer[z])

    def phase1(i):
        C1(i).wait_recv()
        tab[4 * i + 1, 0:T1] = tab[4 * i + 1, 0:T1] + recvC1[i]
        for d in range(1, D):
            A1(i, d).start()
        B1(i).start()

    def core2(i):
        C2(i).wait_recv()
        tab[4 * i + 3, 0:T2] = tab[4 * i + 3, 0:T2] + recvC2[i]

    def phase2(i):
        x0 = pl.ds(D * hb, hb)
        for d in range(1, D):
            A1(i, d).wait_recv()
            tab[4 * i + 3, 0:hb] = tab[4 * i + 3, 0:hb] + rA1[i, d - 1, hb:2 * hb]
        A2(i).start()
        B1(i).wait_recv()
        for d in range(1, D):
            tab[4 * i + 3, d * hb:(d + 1) * hb] = tab[4 * i + 3, d * hb:(d + 1) * hb] + rB1[i, d * hb:(d + 1) * hb]
            B2(i, d).start()
        extra = rA1[i, 0, 0:hb]
        for d in range(2, D):
            extra = extra + rA1[i, d - 1, 0:hb]
        tab[4 * i + 3, x0] = tab[4 * i + 3, x0] + extra
        b0 = pl.ds((D + 1) * hb, hb)
        tab[4 * i + 3, b0] = tab[4 * i + 3, b0] + rB1[i, 0:hb]

    def phase3(i):
        x0 = pl.ds(D * hb, hb)
        b0 = pl.ds((D + 1) * hb, hb)
        A2(i).wait_recv()
        tab[4 * i + 3, x0] = tab[4 * i + 3, x0] + rA2[i]
        for d in range(1, D):
            B2(i, d).wait_recv()
            tab[4 * i + 3, b0] = tab[4 * i + 3, b0] + rB2[i, d - 1]
        for z in range(1, Z):
            if isinstance(i, int):
                if i == Z - 1 - z:
                    ZC(i, z).start()
                continue

            @pl.when(i == Z - 1 - z)
            def _():
                ZC(i, z).start()

    def DC(d):
        return rcopy(c0.at[d], cD.at[d - 1], scD.at[d - 1], tcD.at[d - 1], dpeer[d])

    def XC():
        return rcopy(cX, cXr, scX, tcX, xpeer)

    def ZCc(z):
        return rcopy(cZ, cZr.at[z - 1], scZ.at[z - 1], tcZ.at[z - 1], zpeer[z])

    def count_step(i):
        @pl.when(i == 0)
        def _():
            cc.wait_recv()
            for d in range(D):
                c0[d] = c0[d] + cR[d]
            for d in range(1, D):
                DC(d).start()

        @pl.when(i == 1)
        def _():
            v = c0[0]
            for d in range(1, D):
                DC(d).wait_recv()
                v = v + cD[d - 1]
            cX[...] = v
            XC().start()

        @pl.when(i == 2)
        def _():
            XC().wait_recv()
            cZ[...] = cX[0:Z] + cXr[Z:2 * Z]
            for z in range(1, Z):
                ZCc(z).start()

    @pl.loop(0, 4 * Z)
    def _(t):
        i, j = t // 4, t % 4
        tab[t] = tile((2 * i + 1 - j % 2) * stage + (j // 2) * T1, max(T1, T2))

        @pl.when(j == 0)
        def _():
            C1(i).start()

        @pl.when((j == 0) & (i >= 1))
        def _():
            core2(i - 1)

        @pl.when(j == 1)
        def _():
            phase1(i)
            count_step(i)

        @pl.when(j == 2)
        def _():
            C2(i).start()

        @pl.when((j == 2) & (i >= 1))
        def _():
            phase2(i - 1)

        @pl.when((j == 3) & (i >= 2))
        def _():
            phase3(i - 2)

    core2(Z - 1)
    phase2(Z - 1)
    phase3(Z - 2)
    phase3(Z - 1)
    cf = cZ[0:1, :]
    for z in range(1, Z):
        ZCc(z).wait_recv()
        cf = cf + cZr[z - 1, z:z + 1, :]
    cout_ref[...] = cf
    spread = jnp.broadcast_to(jnp.maximum(cf, 1.0), (kpd, kpd))
    eye = lax.broadcasted_iota(jnp.int32, (kpd, kpd), 0) == lax.broadcasted_iota(jnp.int32, (kpd, kpd), 1)
    col = jnp.sum(jnp.where(eye, spread, 0.0), axis=1, keepdims=True)
    tot = tab[4 * Z - 1, D * hb:(D + 2) * hb]
    for i in range(Z - 1):
        ZC(i, Z - 1 - i).wait_recv()
        tot = tot + rZ[i]
    out_ref[...] = tot / col

    cc.wait_send()
    for d in range(1, D):
        DC(d).wait_send()
    XC().wait_send()
    for z in range(1, Z):
        ZCc(z).wait_send()
        ZC(Z - 1 - z, z).wait_send()

    @pl.loop(0, Z)
    def _(i):
        C1(i).wait_send()
        C2(i).wait_send()
        for d in range(1, D):
            A1(i, d).wait_send()
            B2(i, d).wait_send()
        B1(i).wait_send()
        A2(i).wait_send()


def per_device(facts, row_owner, key_offset):
    n_dom, n_rep = lax.axis_size("dom"), lax.axis_size("rep")
    rows, M = facts.shape
    D, Z = n_dom // 2, n_rep // 2
    kpd = KEYS // (n_dom * n_rep)
    hb = kpd // 2
    T1, T2 = (3 * D - 2) * hb, (D + 2) * hb
    chunk = min(1024, rows)

    def vm(*shape, dtype=F32):
        return pltpu.VMEM(shape, dtype)

    def dma(*shape):
        return [pltpu.SemaphoreType.DMA(shape)] * 2 if shape else [pltpu.SemaphoreType.DMA] * 2

    scratch = [
        vm(1, rows, dtype=jnp.int32), vm(1, rows, dtype=jnp.int32), vm(1, rows, dtype=jnp.int32),
        vm(rows, M), vm(rows, M, dtype=BF16), vm(rows, M, dtype=BF16),
        vm(4 * Z, max(T1, T2), M), vm(Z, T1, M), vm(Z, T2, M),
        vm(Z, D - 1, 2 * hb, M), vm(Z, D * hb, M), vm(Z, hb, M), vm(Z, D - 1, hb, M), vm(Z - 1, 2 * hb, M),
        vm(D, 2 * Z, kpd), vm(D, 2 * Z, kpd), vm(D, 2 * Z, kpd), vm(D - 1, 2 * Z, kpd),
        vm(2 * Z, kpd), vm(2 * Z, kpd), vm(Z, kpd), vm(Z - 1, Z, kpd),
        pltpu.SemaphoreType.DMA((rows // chunk,)), pltpu.SemaphoreType.DMA((2,)),
        *dma(Z), *dma(Z), *dma(Z, D - 1), *dma(Z), *dma(Z), *dma(Z, D - 1), *dma(Z - 1),
        *dma(), *dma(D - 1), *dma(), *dma(Z - 1),
    ]
    vmem = pl.BlockSpec(memory_space=pltpu.VMEM)
    means, counts = pl.pallas_call(
        functools.partial(kernel, D, Z, hb, rows, M, chunk),
        out_shape=(jax.ShapeDtypeStruct((kpd, M), F32), jax.ShapeDtypeStruct((1, kpd), F32)),
        in_specs=[pl.BlockSpec(memory_space=pl.ANY)] * 3,
        out_specs=(vmem, vmem),
        scratch_shapes=scratch,
        compiler_params=pltpu.CompilerParams(
            collective_id=0, has_side_effects=True, vmem_limit_bytes=50 * 1024 * 1024
        ),
    )(row_owner.reshape(1, rows), key_offset.reshape(1, rows), facts)
    return means, counts.reshape(kpd)


def solution(mesh):
    placed = (P(("dom", "rep"), None), P(("dom", "rep"), None), P(("dom", "rep")))
    return jax.shard_map(
        per_device,
        mesh=mesh,
        in_specs=placed,
        out_specs=(P(("dom", "rep"), None), P(("dom", "rep"))),
        check_vma=False,
    )
```

profile of v0, /device:TPU:0, one launch (start us, length us, event | category | flops | bytes accessed | tf_op | source)
XLA Modules:
  0.0 40.4 jit_solution(13503178145475038877)
XLA Ops:
  0.6 0.0 copy-start
  0.6 0.7 %copy-done = s32[4096,1]{0,1:T(1,128)S(1)} copy-done((s32[4096,1]{0,1:T(1,128)S(1)}, s32[4096,1]{0,1:T(1,128)}, u32[]{:S(2)}) %copy-start) | copy-done | bytes 16408
  1.3 0.0 copy-start.1
  1.4 0.7 %copy-done.1 = s32[4096]{0:T(1024)S(1)} copy-done((s32[4096]{0:T(1024)S(1)}, s32[4096]{0:T(1024)}, u32[]{:S(2)}) %copy-start.1) | copy-done | bytes 16408
  2.1 37.2 %shard_map.50 = (f32[128,256]{1,0:T(8,128)S(1)}, f32[1,128]{1,0:T(1,128)S(1)}) custom-call(s32[1,4096]{1,0:T(1,128)S(1)} %bitcast.3, s32[1,4096]{1,0:T(1,128)S(1)} %bitcast.4, f32[4096,256]{1,0:T(8,128)} %facts_ref.1), custom_call_target="tpu_custom_call" | custom-call | tf_op jit(solution)/shard_map/pallas_call | solution.py:310
  39.3 0.7 %copy.7 = f32[128,256]{1,0:T(8,128)} copy(f32[128,256]{1,0:T(8,128)S(1)} %get-tuple-element.8) | data formatting | bytes 262144
  39.9 0.5 %copy.8 = f32[128]{0:T(128)} copy(f32[128]{0:T(128)S(1)} %bitcast.5) | data formatting | bytes 1024
Async XLA Ops:
  0.6 0.7 %copy-start = (s32[4096,1]{0,1:T(1,128)S(1)}, s32[4096,1]{0,1:T(1,128)}, u32[]{:S(2)}) copy-start(s32[4096,1]{0,1:T(1,128)} %param.4) | copy-start | bytes 49156
  1.3 0.7 %copy-start.1 = (s32[4096]{0:T(1024)S(1)}, s32[4096]{0:T(1024)}, u32[]{:S(2)}) copy-start(s32[4096]{0:T(1024)} %param.5) | copy-start | bytes 49156
where the time goes:
time: 40.8 us; the launch traced here: 40.4 us
  Pallas kernels  37.2 us (91%)
  local copies, waits for them, and re-layouts  2.6 us (6%)
  between operations  0.65 us (2%)
    pallas_call x1, Pallas kernels, per_device(): pl.pallas_call(functools.partial(kernel, D, Z, hb, rows, M, chunk), out_s...  37.2 us
    unnamed x6, local copies, waits for them, and re-layouts  2.6 us

commit v1 on v0

--- a/solution.py
+++ b/solution.py
@@ -11,6 +11,8 @@
 MESH = pl.DeviceIdType.MESH
 F32 = jnp.float32
 BF16 = jnp.bfloat16
+LANES = 128
+TABLES = 4
 
 
 def flip(index, bits):
@@ -22,25 +24,30 @@
     return index
 
 
-def kernel(D, Z, hb, rows, M, chunk, owner_hbm, offset_hbm, facts_ref, out_ref, cout_ref,
-           owner_ref, offset_ref, lab_ref, fbuf, high, low, tab, recvC1, recvC2,
-           rA1, rB1, rA2, rB2, rZ,
-           c0, cS, cR, cD, cX, cXr, cZ, cZr, fsem, isem,
-           sC1, tC1, sC2, tC2, sA1, tA1, sB1, tB1, sA2, tA2, sB2, tB2, sZ, tZ,
-           scC, tcC, scD, tcD, scX, tcX, scZ, tcZ):
+def table_rows(D, Z, hb, me_d, me_r, owner, offset):
+    kpd = 2 * hb
+    rel = owner ^ me_d
+    dc, d = rel & 1, rel >> 1
+    i = offset & (kpd - 1)
+    rr = (offset >> (kpd.bit_length() - 1)) ^ me_r
+    x, z = rr & 1, rr >> 1
+    blk_a = jnp.where(d > 0, 2 * (d - 1) + x, jnp.where(x > 0, 3 * D - 2, 4 * D - 2))
+    blk_b = jnp.where(x > 0, 2 * (D - 1) + d, jnp.where(d > 0, 3 * D - 2 + d, 4 * D - 1))
+    blk = jnp.where(i >= hb, blk_b, blk_a)
+    lab = (((Z - 1 - z) * 2 + dc) * (4 * D) + blk) * hb + (i & (hb - 1))
+    crow = ((dc * D + d) * 2 + x) * Z + z
+    return lab, crow, i
+
+
+def scatter(D, Z, hb, rows, owner_hbm, offset_hbm, facts_hbm, *refs):
+    tabs, refs = refs[:TABLES], refs[TABLES:]
+    owner_ref, offset_ref, lab_ref, at_ref, fbuf, isem, lsem, fsem = refs
     me_d, me_r = lax.axis_index("dom"), lax.axis_index("rep")
-    T1, T2 = (3 * D - 2) * hb, (D + 2) * hb
-    stage = 4 * D * hb
-    core = (flip(me_d, 1), me_r)
-    dpeer = [None] + [(flip(me_d, 2 * d), me_r) for d in range(1, D)]
-    xpeer = (me_d, flip(me_r, 1))
-    zpeer = [None] + [(me_d, flip(me_r, 2 * z)) for z in range(1, Z)]
-    peers = [core] + dpeer[1:] + [xpeer] + zpeer[1:]
-
-    nchunks = rows // chunk
+    nchunks = fsem.shape[0]
+    words = 2 * rows // nchunks
     loads = [
         pltpu.make_async_copy(
-            facts_ref.at[pl.ds(k * chunk, chunk)], fbuf.at[pl.ds(k * chunk, chunk)], fsem.at[k]
+            facts_hbm.at[pl.ds(k * words, words)], fbuf.at[pl.ds(k * words, words)], fsem.at[k]
         )
         for k in range(nchunks)
     ]
@@ -50,6 +57,58 @@
     ]
     for ld in ints + loads:
         ld.start()
+    for ld in ints:
+        ld.wait()
+    lab_ref[...] = 2 * table_rows(D, Z, hb, me_d, me_r, owner_ref[...], offset_ref[...])[0]
+    labels = pltpu.make_async_copy(lab_ref, at_ref, lsem)
+    labels.start()
+
+    @pl.loop(0, 2 * KEYS // 128)
+    def _(i):
+        at = pl.ds(pl.multiple_of(i * 128, 128), 128)
+        for tab in tabs:
+            tab[at, :] = jnp.zeros((128, LANES), F32)
+
+    labels.wait()
+    group = rows // nchunks // LANES
+    for k in range(nchunks):
+        loads[k].wait()
+
+        @pl.loop(0, group)
+        def _(g):
+            base = pl.multiple_of((k * group + g) * 2 * LANES, 2 * LANES)
+            for r in range(0, LANES, TABLES):
+                at = [pl.multiple_of(at_ref[k * group + g, r + u], 2) for u in range(TABLES)]
+                row = [fbuf[pl.ds(base + 16 * ((r + u) // 8) + (r + u) % 8, 2, stride=8), :] for u in range(TABLES)]
+                row = [tabs[u][pl.ds(at[u], 2), :] + row[u] for u in range(TABLES)]
+                for u in range(TABLES):
+                    tabs[u][pl.ds(at[u], 2), :] = row[u]
+
+
+def kernel(D, Z, hb, rows, owner_hbm, offset_hbm, *refs):
+    tabs, refs = refs[:TABLES], refs[TABLES:]
+    (out_ref, cout_ref, owner_ref, offset_ref, tab, recvC1, recvC2,
+     rA1, rB1, rA2, rB2, rZ,
+     c0, cS, cR, cD, cX, cXr, cZ, cZr, isem,
+     sC1, tC1, sC2, tC2, sA1, tA1, sB1, tB1, sA2, tA2, sB2, tB2, sZ, tZ,
+     scC, tcC, scD, tcD, scX, tcX, scZ, tcZ) = refs
+    me_d, me_r = lax.axis_index("dom"), lax.axis_index("rep")
+    kpd = 2 * hb
+    hb = 2 * hb
+    T1, T2 = (3 * D - 2) * hb, (D + 2) * hb
+    stage = 4 * D * hb
+    core = (flip(me_d, 1), me_r)
+    dpeer = [None] + [(flip(me_d, 2 * d), me_r) for d in range(1, D)]
+    xpeer = (me_d, flip(me_r, 1))
+    zpeer = [None] + [(me_d, flip(me_r, 2 * z)) for z in range(1, Z)]
+    peers = [core] + dpeer[1:] + [xpeer] + zpeer[1:]
+
+    ints = [
+        pltpu.make_async_copy(owner_hbm, owner_ref, isem.at[0]),
+        pltpu.make_async_copy(offset_hbm, offset_ref, isem.at[1]),
+    ]
+    for ld in ints:
+        ld.start()
     barrier = pltpu.get_barrier_semaphore()
     for p in peers:
         pl.semaphore_signal(barrier, inc=1, device_id=p, device_id_type=MESH)
@@ -59,57 +118,35 @@
             src_ref=src, dst_ref=dst, send_sem=s, recv_sem=t, device_id=dev, device_id_type=MESH
         )
 
-    nrow = 4 * D * Z
-    kpd = 2 * hb
-    for ld in ints:
-        ld.wait()
-    rel = owner_ref[...] ^ me_d
-    dc, d = rel & 1, rel >> 1
-    offset = offset_ref[...]
-    i = offset & (kpd - 1)
-    rr = (offset >> (kpd.bit_length() - 1)) ^ me_r
-    x, z = rr & 1, rr >> 1
-    ii = i & (hb - 1)
-    blk_a = jnp.where(d > 0, 2 * (d - 1) + x, jnp.where(x > 0, 3 * D - 2, 4 * D - 2))
-    blk_b = jnp.where(x > 0, 2 * (D - 1) + d, jnp.where(d > 0, 3 * D - 2 + d, 4 * D - 1))
-    blk = jnp.where(i >= hb, blk_b, blk_a)
-    lab_ref[...] = (((Z - 1 - z) * 2 + dc) * (4 * D) + blk) * hb + ii
-    crow = ((dc * D + d) * 2 + x) * Z + z
-    hot_r = jnp.where(lax.broadcasted_iota(jnp.int32, (nrow, rows), 0) == crow, 1.0, 0.0).astype(BF16)
-    hot_c = jnp.where(lax.broadcasted_iota(jnp.int32, (kpd, rows), 0) == i, 1.0, 0.0).astype(BF16)
-    cnt = lax.dot_general(hot_r, hot_c, (((1,), (1,)), ((), ())), preferred_element_type=F32)
-    half = nrow // 2
-    for d in range(D):
-        c0[d] = cnt[d * 2 * Z:(d + 1) * 2 * Z]
-        cS[d] = cnt[half + d * 2 * Z:half + (d + 1) * 2 * Z]
-
-    for k in range(nchunks):
-        loads[k].wait()
-
-        @pl.loop(0, chunk // 256)
-        def _(j):
-            at = pl.multiple_of(k * chunk + j * 256, 256)
-            v = fbuf[pl.ds(at, 256), :]
-            hi = v.astype(BF16)
-            high[pl.ds(at, 256), :] = hi
-            low[pl.ds(at, 256), :] = (v - hi.astype(F32)).astype(BF16)
-
-    pl.semaphore_wait(barrier, len(peers))
+    def tile(t):
+        i, j = t // 4, t % 4
+        start = (2 * i + 1 - j % 2) * stage + (j // 2) * T1
+        size = max(T1, T2)
+        step = min(size, 128)
+
+        @pl.loop(0, size // step)
+        def _(n):
+            at = pl.ds(pl.multiple_of(start + n * step, 8), step)
+            v = tabs[0][at, :]
+            for other in tabs[1:]:
+                v = v + other[at, :]
+            tab[t, pl.ds(pl.multiple_of(n * step, 8), step), :] = v
+
+    def counts():
+        for ld in ints:
+            ld.wait()
+        nrow = 4 * D * Z
+        _, crow, i = table_rows(D, Z, kpd // 2, me_d, me_r, owner_ref[...], offset_ref[...])
+        hot_r = jnp.where(lax.broadcasted_iota(jnp.int32, (nrow, rows), 0) == crow, 1.0, 0.0).astype(BF16)
+        hot_c = jnp.where(lax.broadcasted_iota(jnp.int32, (kpd, rows), 0) == i, 1.0, 0.0).astype(BF16)
+        cnt = lax.dot_general(hot_r, hot_c, (((1,), (1,)), ((), ())), preferred_element_type=F32)
+        half = nrow // 2
+        for d in range(D):
+            c0[d] = cnt[d * 2 * Z:(d + 1) * 2 * Z]
+            cS[d] = cnt[half + d * 2 * Z:half + (d + 1) * 2 * Z]
+        cc.start()
+
     cc = rcopy(cS, cR, scC, tcC, core)
-    cc.start()
-
-    def tile(start, size):
-        rel = lab_ref[...] - start
-        total = None
-        for k in range(nchunks):
-            part = rel[:, k * chunk:(k + 1) * chunk]
-            hot = jnp.where(lax.broadcasted_iota(jnp.int32, (size, chunk), 0) == part, 1.0, 0.0).astype(BF16)
-            at = slice(k * chunk, (k + 1) * chunk)
-            o = jnp.dot(hot, high[at, :], preferred_element_type=F32) + jnp.dot(
-                hot, low[at, :], preferred_element_type=F32
-            )
-            total = o if total is None else total + o
-        return total
 
     def C1(i):
         return rcopy(tab.at[4 * i, pl.ds(0, T1)], recvC1.at[i], sC1.at[i], tC1.at[i], core)
@@ -213,17 +250,19 @@
             for z in range(1, Z):
                 ZCc(z).start()
 
-    @pl.loop(0, 4 * Z)
+    tile(0)
+    pl.semaphore_wait(barrier, len(peers))
+    C1(0).start()
+    counts()
+
+    @pl.loop(1, 4 * Z)
     def _(t):
         i, j = t // 4, t % 4
-        tab[t] = tile((2 * i + 1 - j % 2) * stage + (j // 2) * T1, max(T1, T2))
+        tile(t)
 
         @pl.when(j == 0)
         def _():
             C1(i).start()
-
-        @pl.when((j == 0) & (i >= 1))
-        def _():
             core2(i - 1)
 
         @pl.when(j == 1)
@@ -259,7 +298,10 @@
     for i in range(Z - 1):
         ZC(i, Z - 1 - i).wait_recv()
         tot = tot + rZ[i]
-    out_ref[...] = tot / col
+    rZ[Z - 1] = tot
+    last = rZ.at[Z - 1]
+    out_ref[:, 0:LANES] = last[pl.ds(0, kpd, stride=2), :] / col
+    out_ref[:, LANES:2 * LANES] = last[pl.ds(1, kpd, stride=2), :] / col
 
     cc.wait_send()
     for d in range(1, D):
@@ -286,8 +328,8 @@
     D, Z = n_dom // 2, n_rep // 2
     kpd = KEYS // (n_dom * n_rep)
     hb = kpd // 2
-    T1, T2 = (3 * D - 2) * hb, (D + 2) * hb
-    chunk = min(1024, rows)
+    T1, T2 = 2 * (3 * D - 2) * hb, 2 * (D + 2) * hb
+    nchunks = 2
 
     def vm(*shape, dtype=F32):
         return pltpu.VMEM(shape, dtype)
@@ -295,28 +337,49 @@
     def dma(*shape):
         return [pltpu.SemaphoreType.DMA(shape)] * 2 if shape else [pltpu.SemaphoreType.DMA] * 2
 
+    I32 = jnp.int32
+    pin = pltpu.with_memory_space_constraint
+    hbm = pl.BlockSpec(memory_space=pltpu.HBM)
+    vmem = pl.BlockSpec(memory_space=pltpu.VMEM)
+    by_tile = facts.reshape(rows // 8, 8, 2, LANES).transpose(0, 2, 1, 3).reshape(2 * rows, LANES)
+    square = (rows // LANES, LANES)
+    tables = pl.pallas_call(
+        functools.partial(scatter, D, Z, hb, rows),
+        out_shape=[vm(2 * KEYS, LANES)] * TABLES,
+        in_specs=[hbm] * 3,
+        out_specs=[vmem] * TABLES,
+        scratch_shapes=[
+            vm(*square, dtype=I32), vm(*square, dtype=I32), vm(*square, dtype=I32), pltpu.SMEM(square, I32),
+            vm(2 * rows, LANES),
+            pltpu.SemaphoreType.DMA((2,)), pltpu.SemaphoreType.DMA, pltpu.SemaphoreType.DMA((nchunks,)),
+        ],
+        compiler_params=pltpu.CompilerParams(vmem_limit_bytes=24 * 1024 * 1024),
+    )(*(pin(a, pltpu.HBM) for a in (row_owner.reshape(square), key_offset.reshape(square), by_tile)))
+
+    h = 2 * hb
     scratch = [
-        vm(1, rows, dtype=jnp.int32), vm(1, rows, dtype=jnp.int32), vm(1, rows, dtype=jnp.int32),
-        vm(rows, M), vm(rows, M, dtype=BF16), vm(rows, M, dtype=BF16),
-        vm(4 * Z, max(T1, T2), M), vm(Z, T1, M), vm(Z, T2, M),
-        vm(Z, D - 1, 2 * hb, M), vm(Z, D * hb, M), vm(Z, hb, M), vm(Z, D - 1, hb, M), vm(Z - 1, 2 * hb, M),
+        vm(1, rows, dtype=I32), vm(1, rows, dtype=I32),
+        vm(4 * Z, max(T1, T2), LANES), vm(Z, T1, LANES), vm(Z, T2, LANES),
+        vm(Z, D - 1, 2 * h, LANES), vm(Z, D * h, LANES), vm(Z, h, LANES), vm(Z, D - 1, h, LANES), vm(Z, 2 * h, LANES),
         vm(D, 2 * Z, kpd), vm(D, 2 * Z, kpd), vm(D, 2 * Z, kpd), vm(D - 1, 2 * Z, kpd),
         vm(2 * Z, kpd), vm(2 * Z, kpd), vm(Z, kpd), vm(Z - 1, Z, kpd),
-        pltpu.SemaphoreType.DMA((rows // chunk,)), pltpu.SemaphoreType.DMA((2,)),
+        pltpu.SemaphoreType.DMA((2,)),
         *dma(Z), *dma(Z), *dma(Z, D - 1), *dma(Z), *dma(Z), *dma(Z, D - 1), *dma(Z - 1),
         *dma(), *dma(D - 1), *dma(), *dma(Z - 1),
     ]
-    vmem = pl.BlockSpec(memory_space=pltpu.VMEM)
     means, counts = pl.pallas_call(
-        functools.partial(kernel, D, Z, hb, rows, M, chunk),
+        functools.partial(kernel, D, Z, hb, rows),
         out_shape=(jax.ShapeDtypeStruct((kpd, M), F32), jax.ShapeDtypeStruct((1, kpd), F32)),
-        in_specs=[pl.BlockSpec(memory_space=pl.ANY)] * 3,
+        in_specs=[hbm] * 2 + [vmem] * TABLES,
         out_specs=(vmem, vmem),
         scratch_shapes=scratch,
         compiler_params=pltpu.CompilerParams(
-            collective_id=0, has_side_effects=True, vmem_limit_bytes=50 * 1024 * 1024
+            collective_id=0, has_side_effects=True, vmem_limit_bytes=24 * 1024 * 1024
         ),
-    )(row_owner.reshape(1, rows), key_offset.reshape(1, rows), facts)
+    )(
+        pin(row_owner.reshape(1, rows), pltpu.HBM), pin(key_offset.reshape(1, rows), pltpu.HBM),
+        *(pin(table, pltpu.VMEM) for table in tables),
+    )
     return means, counts.reshape(kpd)
 
 

time: 40.8 us -> 41.6 us (1.020)
  Pallas kernels: 37.2 us -> 39.6 us
  local copies, waits for them, and re-layouts: 2.6 us -> 1.17 us
    pallas_call x1 -> x2, Pallas kernels: 37.2 us -> 39.6 us  [the longest x1 31.6 us: per_device(): pl.pallas_call(functools.partial(kernel, D, Z, hb, rows), out_shape=(jax....]
    unnamed x6 -> x2, local copies, waits for them, and re-layouts: 2.6 us -> 1.17 us
where the time goes in v1:
time: 41.6 us; the launch traced here: 41.4 us
  Pallas kernels  39.6 us (95%)
  local copies, waits for them, and re-layouts  1.17 us (3%)
  between operations  0.65 us (2%)
    pallas_call x1, Pallas kernels, per_device(): pl.pallas_call(functools.partial(kernel, D, Z, hb, rows), out_shape=(jax....  31.6 us
    pallas_call x1, Pallas kernels, per_device(): pl.pallas_call(functools.partial(scatter, D, Z, hb, rows), out_shape=[vm(...  8.01 us
    unnamed x2, local copies, waits for them, and re-layouts  1.17 us

profile of v1, /device:TPU:0, one launch (start us, length us, event | category | flops | bytes accessed | tf_op | source)
XLA Modules:
  0.0 41.4 jit_solution(13603546752082311023)
XLA Ops:
  0.6 8.0 %shard_map.50 = (f32[8192,128]{1,0:T(8,128)S(1)}, f32[8192,128]{1,0:T(8,128)S(1)}, f32[8192,128]{1,0:T(8,128)S(1)}, f32[8192,128]{1,0:T(8,128)S(1)}) custom-call(s32[32,128]{1,0:T(8,128)} %bitcast.12, s32[32,128]{1,0:T(8,128)} %bitcast.14, f32[8192,128]{1,0:T(8,128)} %bitcast.11), custom_call_target="tpu_custom_call" | custom-call | tf_op jit(solution)/shard_map/pallas_call | solution.py:346
  8.6 31.6 %shard_map.51 = (f32[128,256]{1,0:T(8,128)S(1)}, f32[1,128]{1,0:T(1,128)S(1)}) custom-call(s32[1,4096]{1,0:T(1,128)} %bitcast.13, s32[1,4096]{1,0:T(1,128)} %bitcast.15, f32[8192,128]{1,0:T(8,128)S(1)} %get-tuple-element.8.refs_0_, f32[8192,128]{1,0:T(8,128)S(1)} %get-tuple-element.9.refs_1_, f32[8192,128]{1,0:T(8,128)S(1)} %get-tuple-element.10.refs_2_, ...), custom_call_target="tpu_custom_call" | custom-call | tf_op jit(solution)/shard_map/pallas_call | solution.py:370
  40.2 0.7 %copy.7 = f32[128,256]{1,0:T(8,128)} copy(f32[128,256]{1,0:T(8,128)S(1)} %get-tuple-element.16) | data formatting | bytes 262144
  40.9 0.5 %copy.8 = f32[128]{0:T(128)} copy(f32[128]{0:T(128)S(1)} %bitcast.10) | data formatting | bytes 1024

commit v2 on v1

v2 whole, which is shorter than its diff:
```python
import functools

import jax
import jax.numpy as jnp
from jax import lax
from jax.experimental import pallas as pl
from jax.experimental.pallas import tpu as pltpu
from jax.sharding import PartitionSpec as P

KEYS = 4096
MESH = pl.DeviceIdType.MESH
F32 = jnp.float32
BF16 = jnp.bfloat16
LANES = 128
TABLES = 4
PAIR = 2
SIDE = 28


def flip(index, bits):
    at = 1
    while at <= bits:
        if bits & at:
            index = index + at * (1 - 2 * ((index // at) % 2))
        at *= 2
    return index


def log2(n):
    return n.bit_length() - 1


def routes(n_dom, n_rep, kpd):
    x, y = (0, 1), (2, 0)
    rest = [(1 << b, 0) for b in range(2, log2(n_dom))] + [(0, 1 << b) for b in range(1, log2(n_rep))]
    side = kpd * SIDE // 128 // 4 * 4
    parts = [(0, kpd - side, ([x, y, *rest], [y, x, *rest]))]
    if side:
        parts.append((kpd - side, side, ([*rest, y, x], [*rest, x, y])))
    return parts


def label(orders, n_dom, n_rep, me_d, me_r, owner, rep):
    rel_d, rel_r = owner ^ me_d, rep ^ me_r
    found = []
    for order in orders:
        r = rel_d & 1
        for bit_d, bit_r in order:
            bit = rel_d >> log2(bit_d) if bit_d else rel_r >> log2(bit_r)
            r = 2 * r + (bit & 1)
        found.append(r)
    return jnp.where((owner & 1) == 0, found[0], found[1])


def scatter(parts, n_dom, n_rep, rows, owner_hbm, offset_hbm, owner_row_hbm, offset_row_hbm, facts_hbm, *refs):
    tabs, refs = refs[:TABLES], refs[TABLES:]
    cnt_ref, owner_ref, offset_ref, owner_row, offset_row, lab_ref, at_ref, fbuf, isem, lsem, fsem = refs
    me_d, me_r = lax.axis_index("dom"), lax.axis_index("rep")
    blocks = n_dom * n_rep // 2
    kpd = KEYS // (2 * blocks)
    nchunks = fsem.shape[0]
    words = 2 * rows // nchunks
    ints = [
        pltpu.make_async_copy(src, dst, isem.at[k])
        for k, (src, dst) in enumerate(
            [(owner_hbm, owner_ref), (offset_hbm, offset_ref), (owner_row_hbm, owner_row), (offset_row_hbm, offset_row)]
        )
    ]
    loads = [
        pltpu.make_async_copy(
            facts_hbm.at[pl.ds(k * words, words)], fbuf.at[pl.ds(k * words, words)], fsem.at[k]
        )
        for k in range(nchunks)
    ]
    for ld in ints + loads:
        ld.start()

    def clear(first, last):
        @pl.loop(0, KEYS // 64)
        def _(i):
            at = pl.ds(pl.multiple_of(i * 128, 128), 128)
            for tab in tabs[first:last]:
                tab[at, :] = jnp.zeros((128, LANES), F32)

    clear(0, TABLES // 2)
    for ld in ints[:2]:
        ld.wait()
    owner, offset = owner_ref[...], offset_ref[...]
    i, base, word = offset & (kpd - 1), 0, None
    for first, keys, orders in parts:
        r = label(orders, n_dom, n_rep, me_d, me_r, owner, offset >> log2(kpd))
        at = base + 2 * (r * keys + i - first)
        word = at if word is None else jnp.where(i >= first, at, word)
        base += 4 * blocks * keys
    lab_ref[...] = word
    labels = pltpu.make_async_copy(lab_ref, at_ref, lsem)
    labels.start()
    clear(TABLES // 2, TABLES)
    for ld in ints[2:]:
        ld.wait()
    owner, offset = owner_row[...], offset_row[...]
    r = label(parts[0][2], n_dom, n_rep, me_d, me_r, owner, offset >> log2(kpd))
    i = offset & (kpd - 1)
    hot_r = jnp.where(lax.broadcasted_iota(jnp.int32, (2 * blocks, rows), 0) == r, 1.0, 0.0).astype(BF16)
    hot_i = jnp.where(lax.broadcasted_iota(jnp.int32, (LANES, rows), 0) == i, 1.0, 0.0).astype(BF16)
    cnt_ref[...] = lax.dot_general(hot_r, hot_i, (((1,), (1,)), ((), ())), preferred_element_type=F32)

    labels.wait()
    group = rows // nchunks // LANES
    for k in range(nchunks):
        loads[k].wait()

        @pl.loop(0, group)
        def _(g):
            base = pl.multiple_of((k * group + g) * 2 * LANES, 2 * LANES)
            mine = at_ref.at[k * group + g]
            for r in range(0, LANES, TABLES * PAIR):
                at = [pl.multiple_of(mine[r + u], 2) for u in range(TABLES * PAIR)]
                row = [fbuf[pl.ds(base + 16 * ((r + u) // 8) + (r + u) % 8, 2, stride=8), :] for u in range(TABLES * PAIR)]
                old = [tabs[u % TABLES][pl.ds(at[u], 2), :] for u in range(TABLES * PAIR)]
                for u in range(TABLES):
                    old[u] = old[u] + row[u]
                    for v in range(u + TABLES, TABLES * PAIR, TABLES):
                        old[v] = jnp.where(at[v] == at[u], old[u], old[v]) + row[v]
                for u in range(TABLES * PAIR):
                    tabs[u % TABLES][pl.ds(at[u], 2), :] = old[u]


def kernel(parts, n_dom, n_rep, cnt_ref, *refs):
    blocks = n_dom * n_rep // 2
    kpd = KEYS // (n_dom * n_rep)
    depth = log2(blocks)
    tabs, (out_ref, cout_ref, final, *refs) = refs[:TABLES], refs[TABLES:]
    buffers = [refs[8 * q:8 * q + 8] for q in range(len(parts))]
    me_d, me_r = lax.axis_index("dom"), lax.axis_index("rep")
    c = me_d % 2
    core = (flip(me_d, 1), me_r)
    peers = [core] + [(flip(me_d, d), flip(me_r, r)) for d, r in parts[0][2][0]]
    barrier = pltpu.get_barrier_semaphore()
    for p in peers:
        pl.semaphore_signal(barrier, inc=1, device_id=p, device_id_type=MESH)

    def rcopy(src, dst, s, t, dev):
        return pltpu.make_async_remote_copy(
            src_ref=src, dst_ref=dst, send_sem=s, recv_sem=t, device_id=dev, device_id_type=MESH
        )

    def across(q, r):
        out, come, _, _, s, t, _, _ = buffers[q]
        return rcopy(out.at[r], come.at[r], s.at[r], t.at[r], core)

    def message(q, r, step):
        _, _, acc, got, _, _, s, t = buffers[q]
        (d0, r0), (d1, r1) = (order[step] for order in parts[q][2])
        peer = ((1 - c) * flip(me_d, d0) + c * flip(me_d, d1), (1 - c) * flip(me_r, r0) + c * flip(me_r, r1))
        return rcopy(acc.at[r], got.at[r], s.at[r], t.at[r], peer)

    bases = [4 * blocks * sum(p[1] for p in parts[:q]) for q in range(len(parts))]

    def local(q, other, r, put):
        words = 2 * parts[q][1]
        at = pl.ds(pl.multiple_of(bases[q] + (other * blocks + r) * words, 8), words)
        v = tabs[0][at, :]
        for tab in tabs[1:]:
            v = v + tab[at, :]
        put(slice(0, words), v)
        if q == 0:
            put(slice(words, words + 1), cnt_ref[pl.ds(other * blocks + r, 1), :])

    def total(q, r, step, put):
        _, come, _, got = buffers[q][:4]
        across(q, r).wait_recv()
        come_from = [come.at[r]]
        for k in range(step):
            at = r + (blocks >> (k + 1))
            message(q, at, k).wait_recv()
            come_from.append(got.at[at])

        def add(rows, v):
            for ref in come_from:
                v = v + ref[rows, :]
            put(rows, v)

        local(q, 0, r, add)

    def into(ref, r):
        def put(rows, v):
            ref[r, rows, :] = v
        return put

    pl.semaphore_wait(barrier, len(peers))

    @pl.loop(0, blocks)
    def _(n):
        for q in range(len(parts)):
            r = blocks - 1 - n
            local(q, 1, r, into(buffers[q][0], r))
            across(q, r).start()

    for step in range(depth):
        size = blocks >> (step + 1)

        @pl.loop(0, size)
        def _(n):
            for q in range(len(parts)):
                r = 2 * size - 1 - n
                total(q, r, step, into(buffers[q][2], r))
                message(q, r, step).start()

    for q in reversed(range(len(parts))):
        first, keys, _ = parts[q]

        def put(rows, v):
            if rows.start < 2 * keys:
                final[2 * first:2 * (first + keys), :] = v
            else:
                final[2 * kpd:2 * kpd + 1, :] = v

        total(q, 0, depth, put)
    cf = final[2 * kpd:2 * kpd + 1, 0:kpd]
    cout_ref[...] = cf
    spread = jnp.broadcast_to(jnp.maximum(cf, 1.0), (kpd, kpd))
    eye = lax.broadcasted_iota(jnp.int32, (kpd, kpd), 0) == lax.broadcasted_iota(jnp.int32, (kpd, kpd), 1)
    col = jnp.sum(jnp.where(eye, spread, 0.0), axis=1, keepdims=True)
    out_ref[:, 0:LANES] = final[pl.ds(0, kpd, stride=2), :] / col
    out_ref[:, LANES:2 * LANES] = final[pl.ds(1, kpd, stride=2), :] / col

    @pl.loop(0, blocks)
    def _(r):
        for q in range(len(parts)):
            across(q, r).wait_send()

    for step in range(depth):
        size = blocks >> (step + 1)

        @pl.loop(size, 2 * size)
        def _(r):
            for q in range(len(parts)):
                message(q, r, step).wait_send()


def per_device(facts, row_owner, key_offset):
    n_dom, n_rep = lax.axis_size("dom"), lax.axis_size("rep")
    rows, M = facts.shape
    blocks = n_dom * n_rep // 2
    kpd = KEYS // (n_dom * n_rep)
    parts = routes(n_dom, n_rep, kpd)
    nchunks = 2

    def vm(*shape, dtype=F32):
        return pltpu.VMEM(shape, dtype)

    def dma(*shape):
        return [pltpu.SemaphoreType.DMA(shape)] * 2 if shape else [pltpu.SemaphoreType.DMA] * 2

    I32 = jnp.int32
    pin = pltpu.with_memory_space_constraint
    hbm = pl.BlockSpec(memory_space=pltpu.HBM)
    vmem = pl.BlockSpec(memory_space=pltpu.VMEM)
    by_tile = facts.reshape(rows // 8, 8, 2, LANES).transpose(0, 2, 1, 3).reshape(2 * rows, LANES)
    square = (rows // LANES, LANES)
    ints = [row_owner.reshape(square), key_offset.reshape(square), row_owner.reshape(1, rows), key_offset.reshape(1, rows)]
    *tables, counted = pl.pallas_call(
        functools.partial(scatter, parts, n_dom, n_rep, rows),
        out_shape=[vm(2 * KEYS, LANES)] * TABLES + [vm(2 * blocks, LANES)],
        in_specs=[hbm] * 5,
        out_specs=[vmem] * (TABLES + 1),
        scratch_shapes=[
            vm(*square, dtype=I32), vm(*square, dtype=I32), vm(1, rows, dtype=I32), vm(1, rows, dtype=I32),
            vm(*square, dtype=I32), pltpu.SMEM(square, I32), vm(2 * rows, LANES),
            pltpu.SemaphoreType.DMA((4,)), pltpu.SemaphoreType.DMA, pltpu.SemaphoreType.DMA((nchunks,)),
        ],
        compiler_params=pltpu.CompilerParams(vmem_limit_bytes=24 * 1024 * 1024),
    )(*(pin(a, pltpu.HBM) for a in ints + [by_tile]))

    scratch = [vm(2 * kpd + 8, LANES)]
    for q, (_, keys, _) in enumerate(parts):
        scratch += [vm(blocks, 2 * keys + (q == 0), LANES)] * 4 + dma(blocks) + dma(blocks)
    means, counts = pl.pallas_call(
        functools.partial(kernel, parts, n_dom, n_rep),
        out_shape=(jax.ShapeDtypeStruct((kpd, M), F32), jax.ShapeDtypeStruct((1, kpd), F32)),
        in_specs=[vmem] * (TABLES + 1),
        out_specs=(vmem, vmem),
        scratch_shapes=scratch,
        compiler_params=pltpu.CompilerParams(
            collective_id=0, has_side_effects=True, vmem_limit_bytes=24 * 1024 * 1024
        ),
    )(*(pin(a, pltpu.VMEM) for a in (counted, *tables)))
    return means, counts.reshape(kpd)


def solution(mesh):
    placed = (P(("dom", "rep"), None), P(("dom", "rep"), None), P(("dom", "rep")))
    return jax.shard_map(
        per_device,
        mesh=mesh,
        in_specs=placed,
        out_specs=(P(("dom", "rep"), None), P(("dom", "rep"))),
        check_vma=False,
    )
```

time: 41.6 us -> 37.8 us (0.909)
  Pallas kernels: 39.6 us -> 35.8 us
    pallas_call x2, Pallas kernels: 39.6 us -> 35.8 us  [the longest x1 28.2 us: per_device(): pl.pallas_call(functools.partial(kernel, parts, n_dom, n_rep), out_shape=...]
where the time goes in v2:
time: 37.8 us; the launch traced here: 37.6 us
  Pallas kernels  35.8 us (95%)
  local copies, waits for them, and re-layouts  1.17 us (3%)
  between operations  0.65 us (2%)
    pallas_call x1, Pallas kernels, per_device(): pl.pallas_call(functools.partial(kernel, parts, n_dom, n_rep), out_shape=...  28.2 us
    pallas_call x1, Pallas kernels, per_device(): pl.pallas_call(functools.partial(scatter, parts, n_dom, n_rep, rows), out...  7.61 us
    unnamed x2, local copies, waits for them, and re-layouts  1.17 us

profile of v2, /device:TPU:0, one launch (start us, length us, event | category | flops | bytes accessed | tf_op | source)
XLA Modules:
  0.0 37.6 jit_solution(13074833779841149553)
XLA Ops:
  0.6 7.6 %shard_map.50 = (f32[8192,128]{1,0:T(8,128)S(1)}, f32[8192,128]{1,0:T(8,128)S(1)}, f32[8192,128]{1,0:T(8,128)S(1)}, f32[8192,128]{1,0:T(8,128)S(1)}, f32[32,128]{1,0:T(8,128)S(1)}) custom-call(s32[32,128]{1,0:T(8,128)} %bitcast.12, s32[32,128]{1,0:T(8,128)} %bitcast.14, s32[1,4096]{1,0:T(1,128)} %bitcast.13, s32[1,4096]{1,0:T(1,128)} %bitcast.15, ...), custom_call_target="tpu_custom_call" | custom-call | tf_op jit(solution)/shard_map/pallas_call | solution.py:263
  8.2 28.2 %shard_map.51 = (f32[128,256]{1,0:T(8,128)S(1)}, f32[1,128]{1,0:T(1,128)S(1)}) custom-call(f32[32,128]{1,0:T(8,128)S(1)} %get-tuple-element.9.cnt_ref, f32[8192,128]{1,0:T(8,128)S(1)} %get-tuple-element.10.refs_0_, f32[8192,128]{1,0:T(8,128)S(1)} %get-tuple-element.11.refs_1_, f32[8192,128]{1,0:T(8,128)S(1)} %get-tuple-element.12.refs_2_, ...), custom_call_target="tpu_custom_call" | custom-call | tf_op jit(solution)/shard_map/pallas_call | solution.py:279
  36.4 0.7 %copy.7 = f32[128,256]{1,0:T(8,128)} copy(f32[128,256]{1,0:T(8,128)S(1)} %get-tuple-element.18) | data formatting | bytes 262144
  37.1 0.5 %copy.8 = f32[128]{0:T(128)} copy(f32[128]{0:T(128)S(1)} %bitcast.10) | data formatting | bytes 1024

commit v3 on v2

--- a/solution.py
+++ b/solution.py
@@ -12,9 +12,13 @@
 F32 = jnp.float32
 BF16 = jnp.bfloat16
 LANES = 128
-TABLES = 4
-PAIR = 2
-SIDE = 28
+TABLES = 6
+LAG = 8
+TURNS = (
+    31, 40, 15, 29, 30, 47, 45, 44, 27, 46, 23, 7, 41, 11, 39, 25,
+    13, 37, 14, 43, 19, 26, 21, 3, 22, 36, 9, 38, 5, 6, 28, 17,
+    42, 10, 12, 18, 24, 35, 8, 1, 20, 2, 34, 33, 4, 32, 16, 0,
+)
 
 
 def flip(index, bits):
@@ -33,11 +37,16 @@
 def routes(n_dom, n_rep, kpd):
     x, y = (0, 1), (2, 0)
     rest = [(1 << b, 0) for b in range(2, log2(n_dom))] + [(0, 1 << b) for b in range(1, log2(n_rep))]
-    side = kpd * SIDE // 128 // 4 * 4
-    parts = [(0, kpd - side, ([x, y, *rest], [y, x, *rest]))]
-    if side:
-        parts.append((kpd - side, side, ([*rest, y, x], [*rest, x, y])))
-    return parts
+    flat, tall = ([x, y, *rest], [y, x, *rest]), ([*rest, y, x], [*rest, x, y])
+    cuts = [kpd * at // 128 // 4 * 4 for at in (0, 52, 100)] + [kpd]
+    ways = [flat, flat, tall]
+    return [(cuts[q], cuts[q + 1] - cuts[q], way) for q, way in enumerate(ways) if cuts[q] < cuts[q + 1]]
+
+
+def turns(blocks, parts):
+    if blocks == 16 and len(parts) == 3:
+        return [divmod(turn, 16) for turn in TURNS]
+    return [(q, r) for r in reversed(range(blocks)) for q in range(len(parts))]
 
 
 def label(orders, n_dom, n_rep, me_d, me_r, owner, rep):
@@ -114,16 +123,10 @@
         def _(g):
             base = pl.multiple_of((k * group + g) * 2 * LANES, 2 * LANES)
             mine = at_ref.at[k * group + g]
-            for r in range(0, LANES, TABLES * PAIR):
-                at = [pl.multiple_of(mine[r + u], 2) for u in range(TABLES * PAIR)]
-                row = [fbuf[pl.ds(base + 16 * ((r + u) // 8) + (r + u) % 8, 2, stride=8), :] for u in range(TABLES * PAIR)]
-                old = [tabs[u % TABLES][pl.ds(at[u], 2), :] for u in range(TABLES * PAIR)]
-                for u in range(TABLES):
-                    old[u] = old[u] + row[u]
-                    for v in range(u + TABLES, TABLES * PAIR, TABLES):
-                        old[v] = jnp.where(at[v] == at[u], old[u], old[v]) + row[v]
-                for u in range(TABLES * PAIR):
-                    tabs[u % TABLES][pl.ds(at[u], 2), :] = old[u]
+            for r in range(LANES):
+                at = pl.ds(pl.multiple_of(mine[r], 2), 2)
+                row = fbuf[pl.ds(base + 16 * (r // 8) + r % 8, 2, stride=8), :]
+                tabs[r % TABLES][at, :] = tabs[r % TABLES][at, :] + row
 
 
 def kernel(parts, n_dom, n_rep, cnt_ref, *refs):
@@ -159,7 +162,7 @@
 
     def local(q, other, r, put):
         words = 2 * parts[q][1]
-        at = pl.ds(pl.multiple_of(bases[q] + (other * blocks + r) * words, 8), words)
+        at = pl.ds(bases[q] + (other * blocks + r) * words, words)
         v = tabs[0][at, :]
         for tab in tabs[1:]:
             v = v + tab[at, :]
@@ -190,22 +193,21 @@
 
     pl.semaphore_wait(barrier, len(peers))
 
-    @pl.loop(0, blocks)
-    def _(n):
-        for q in range(len(parts)):
-            r = blocks - 1 - n
-            local(q, 1, r, into(buffers[q][0], r))
-            across(q, r).start()
-
-    for step in range(depth):
-        size = blocks >> (step + 1)
-
-        @pl.loop(0, size)
-        def _(n):
-            for q in range(len(parts)):
-                r = 2 * size - 1 - n
-                total(q, r, step, into(buffers[q][2], r))
-                message(q, r, step).start()
+    def forward(q, r):
+        step = depth - r.bit_length()
+        total(q, r, step, into(buffers[q][2], r))
+        message(q, r, step).start()
+
+    order = turns(blocks, parts)
+    lead = next(n for n, (q, r) in enumerate(order) if r < blocks // 2)
+    for n, (q, r) in enumerate(order):
+        local(q, 1, r, into(buffers[q][0], r))
+        across(q, r).start()
+        if LAG <= n < lead + LAG:
+            forward(*order[n - LAG])
+    for q, r in order[lead:]:
+        if r:
+            forward(q, r)
 
     for q in reversed(range(len(parts))):
         first, keys, _ = parts[q]
@@ -270,7 +272,7 @@
             vm(*square, dtype=I32), pltpu.SMEM(square, I32), vm(2 * rows, LANES),
             pltpu.SemaphoreType.DMA((4,)), pltpu.SemaphoreType.DMA, pltpu.SemaphoreType.DMA((nchunks,)),
         ],
-        compiler_params=pltpu.CompilerParams(vmem_limit_bytes=24 * 1024 * 1024),
+        compiler_params=pltpu.CompilerParams(vmem_limit_bytes=8 * 1024 * 1024),
     )(*(pin(a, pltpu.HBM) for a in ints + [by_tile]))
 
     scratch = [vm(2 * kpd + 8, LANES)]
@@ -278,12 +280,12 @@
         scratch += [vm(blocks, 2 * keys + (q == 0), LANES)] * 4 + dma(blocks) + dma(blocks)
     means, counts = pl.pallas_call(
         functools.partial(kernel, parts, n_dom, n_rep),
-        out_shape=(jax.ShapeDtypeStruct((kpd, M), F32), jax.ShapeDtypeStruct((1, kpd), F32)),
+        out_shape=(vm(kpd, M), vm(1, kpd)),
         in_specs=[vmem] * (TABLES + 1),
         out_specs=(vmem, vmem),
         scratch_shapes=scratch,
         compiler_params=pltpu.CompilerParams(
-            collective_id=0, has_side_effects=True, vmem_limit_bytes=24 * 1024 * 1024
+            collective_id=0, has_side_effects=True, vmem_limit_bytes=16 * 1024 * 1024
         ),
     )(*(pin(a, pltpu.VMEM) for a in (counted, *tables)))
     return means, counts.reshape(kpd)

time: 37.8 us -> 34 us (0.90)
  Pallas kernels: 35.8 us -> 32 us
    pallas_call x1, Pallas kernels: 28.2 us -> 25.7 us  [per_device(): pl.pallas_call(functools.partial(kernel, parts, n_dom, n_rep), out_shape=...]
    pallas_call x1, Pallas kernels: 7.61 us -> 6.3 us  [per_device(): pl.pallas_call(functools.partial(scatter, parts, n_dom, n_rep, rows), out...]
where the time goes in v3:
time: 34 us; the launch traced here: 33.8 us
  Pallas kernels  32 us (94%)
  local copies, waits for them, and re-layouts  1.17 us (3%)
  between operations  0.65 us (2%)
    pallas_call x1, Pallas kernels, per_device(): pl.pallas_call(functools.partial(kernel, parts, n_dom, n_rep), out_shape=...  25.7 us
    pallas_call x1, Pallas kernels, per_device(): pl.pallas_call(functools.partial(scatter, parts, n_dom, n_rep, rows), out...  6.3 us
    unnamed x2, local copies, waits for them, and re-layouts  1.17 us

profile of v3, /device:TPU:0, one launch (start us, length us, event | category | flops | bytes accessed | tf_op | source)
XLA Modules:
  0.0 33.8 jit_solution(13760434305729043851)
XLA Ops:
  0.6 6.3 %shard_map.50 = (f32[8192,128]{1,0:T(8,128)S(1)}, f32[8192,128]{1,0:T(8,128)S(1)}, f32[8192,128]{1,0:T(8,128)S(1)}, f32[8192,128]{1,0:T(8,128)S(1)}, f32[8192,12...) custom-call(s32[32,128]{1,0:T(8,128)} %bitcast.12, s32[32,128]{1,0:T(8,128)} %bitcast.14, ...), custom_call_target="tpu_custom_call" | custom-call | tf_op jit(solution)/shard_map/pallas_call | solution.py:265
  6.9 25.7 %shard_map.51 = (f32[128,256]{1,0:T(8,128)S(1)}, f32[1,128]{1,0:T(1,128)S(1)}) custom-call(f32[32,128]{1,0:T(8,128)S(1)} %get-tuple-element.11.cnt_ref, f32[8192,128]{1,0:T(8,128)S(1)} %get-tuple-element.12.refs_0_, f32[8192,128]{1,0:T(8,128)S(1)} %get-tuple-element.13.refs_1_, f32[8192,128]{1,0:T(8,128)S(1)} %get-tuple-element.14.refs_2_, ...), custom_call_target="tpu_custom_call" | custom-call | tf_op jit(solution)/shard_map/pallas_call | solution.py:281
  32.7 0.7 %copy.7 = f32[128,256]{1,0:T(8,128)} copy(f32[128,256]{1,0:T(8,128)S(1)} %get-tuple-element.20) | data formatting | bytes 262144
  33.3 0.5 %copy.8 = f32[128]{0:T(128)} copy(f32[128]{0:T(128)S(1)} %bitcast.10) | data formatting | bytes 1024

commit v4 on v3

--- a/solution.py
+++ b/solution.py
@@ -12,7 +12,7 @@
 F32 = jnp.float32
 BF16 = jnp.bfloat16
 LANES = 128
-TABLES = 6
+TABLES = 7
 LAG = 8
 TURNS = (
     31, 40, 15, 29, 30, 47, 45, 44, 27, 46, 23, 7, 41, 11, 39, 25,
@@ -133,7 +133,7 @@
     blocks = n_dom * n_rep // 2
     kpd = KEYS // (n_dom * n_rep)
     depth = log2(blocks)
-    tabs, (out_ref, cout_ref, final, *refs) = refs[:TABLES], refs[TABLES:]
+    tabs, (final, *refs) = refs[:TABLES], refs[TABLES:]
     buffers = [refs[8 * q:8 * q + 8] for q in range(len(parts))]
     me_d, me_r = lax.axis_index("dom"), lax.axis_index("rep")
     c = me_d % 2
@@ -209,6 +209,19 @@
         if r:
             forward(q, r)
 
+    @pl.loop(0, blocks)
+    def _(r):
+        for q in range(len(parts)):
+            across(q, r).wait_send()
+
+    for step in range(depth):
+        size = blocks >> (step + 1)
+
+        @pl.loop(size, 2 * size)
+        def _(r):
+            for q in range(len(parts)):
+                message(q, r, step).wait_send()
+
     for q in reversed(range(len(parts))):
         first, keys, _ = parts[q]
 
@@ -219,26 +232,21 @@
                 final[2 * kpd:2 * kpd + 1, :] = v
 
         total(q, 0, depth, put)
+
+
+def divide(kpd, final, out_hbm, cout_hbm, out_ref, cout_ref, osem):
     cf = final[2 * kpd:2 * kpd + 1, 0:kpd]
     cout_ref[...] = cf
+    copies = [pltpu.make_async_copy(cout_ref, cout_hbm, osem.at[0]), pltpu.make_async_copy(out_ref, out_hbm, osem.at[1])]
+    copies[0].start()
     spread = jnp.broadcast_to(jnp.maximum(cf, 1.0), (kpd, kpd))
     eye = lax.broadcasted_iota(jnp.int32, (kpd, kpd), 0) == lax.broadcasted_iota(jnp.int32, (kpd, kpd), 1)
     col = jnp.sum(jnp.where(eye, spread, 0.0), axis=1, keepdims=True)
     out_ref[:, 0:LANES] = final[pl.ds(0, kpd, stride=2), :] / col
     out_ref[:, LANES:2 * LANES] = final[pl.ds(1, kpd, stride=2), :] / col
-
-    @pl.loop(0, blocks)
-    def _(r):
-        for q in range(len(parts)):
-            across(q, r).wait_send()
-
-    for step in range(depth):
-        size = blocks >> (step + 1)
-
-        @pl.loop(size, 2 * size)
-        def _(r):
-            for q in range(len(parts)):
-                message(q, r, step).wait_send()
+    copies[1].start()
+    for cp in copies:
+        cp.wait()
 
 
 def per_device(facts, row_owner, key_offset):
@@ -275,19 +283,27 @@
         compiler_params=pltpu.CompilerParams(vmem_limit_bytes=8 * 1024 * 1024),
     )(*(pin(a, pltpu.HBM) for a in ints + [by_tile]))
 
-    scratch = [vm(2 * kpd + 8, LANES)]
+    scratch = []
     for q, (_, keys, _) in enumerate(parts):
         scratch += [vm(blocks, 2 * keys + (q == 0), LANES)] * 4 + dma(blocks) + dma(blocks)
-    means, counts = pl.pallas_call(
+    final = pl.pallas_call(
         functools.partial(kernel, parts, n_dom, n_rep),
-        out_shape=(vm(kpd, M), vm(1, kpd)),
+        out_shape=vm(2 * kpd + 8, LANES),
         in_specs=[vmem] * (TABLES + 1),
-        out_specs=(vmem, vmem),
+        out_specs=vmem,
         scratch_shapes=scratch,
         compiler_params=pltpu.CompilerParams(
             collective_id=0, has_side_effects=True, vmem_limit_bytes=16 * 1024 * 1024
         ),
     )(*(pin(a, pltpu.VMEM) for a in (counted, *tables)))
+    means, counts = pl.pallas_call(
+        functools.partial(divide, kpd),
+        out_shape=(jax.ShapeDtypeStruct((kpd, M), F32), jax.ShapeDtypeStruct((1, kpd), F32)),
+        in_specs=[vmem],
+        out_specs=(hbm, hbm),
+        scratch_shapes=[vm(kpd, M), vm(1, kpd), pltpu.SemaphoreType.DMA((2,))],
+        compiler_params=pltpu.CompilerParams(vmem_limit_bytes=4 * 1024 * 1024),
+    )(pin(final, pltpu.VMEM))
     return means, counts.reshape(kpd)
 
 

time: 34 us -> 33 us (0.971)
  local copies, waits for them, and re-layouts: 1.17 us -> 0 us
    unnamed x2 -> x0, local copies, waits for them, and re-layouts: 1.17 us -> none
    pallas_call x0 -> x1, Pallas kernels: none -> 0.77 us  [per_device(): pl.pallas_call(functools.partial(divide, kpd), out_shape=(jax.ShapeDtypeS...]
where the time goes in v4:
time: 33 us; the launch traced here: 32.9 us
  Pallas kernels  32.3 us (98%)
  between operations  0.65 us (2%)
    pallas_call x1, Pallas kernels, per_device(): pl.pallas_call(functools.partial(kernel, parts, n_dom, n_rep), out_shape=...  25.4 us
    pallas_call x1, Pallas kernels, per_device(): pl.pallas_call(functools.partial(scatter, parts, n_dom, n_rep, rows), out...  6.03 us
    pallas_call x1, Pallas kernels, per_device(): pl.pallas_call(functools.partial(divide, kpd), out_shape=(jax.ShapeDtypeS...  0.77 us

profile of v4, /device:TPU:0, one launch (start us, length us, event | category | flops | bytes accessed | tf_op | source)
XLA Modules:
  0.0 32.9 jit_solution(1496130759237549574)
XLA Ops:
  0.6 6.0 %shard_map.50 = (f32[8192,128]{1,0:T(8,128)S(1)}, f32[8192,128]{1,0:T(8,128)S(1)}, f32[8192,128]{1,0:T(8,128)S(1)}, f32[8192,128]{1,0:T(8,128)S(1)}, f32[8192,12...) custom-call(s32[32,128]{1,0:T(8,128)} %bitcast.11, ...), custom_call_target="tpu_custom_call" | custom-call | tf_op jit(solution)/shard_map/pallas_call | solution.py:273
  6.7 25.4 %shard_map.51.final = f32[264,128]{1,0:T(8,128)S(1)} custom-call(f32[32,128]{1,0:T(8,128)S(1)} %get-tuple-element.12.cnt_ref, f32[8192,128]{1,0:T(8,128)S(1)} %get-tuple-element.13.refs_0_, f32[8192,128]{1,0:T(8,128)S(1)} %get-tuple-element.14.refs_1_, f32[8192,128]{1,0:T(8,128)S(1)} %get-tuple-element.15.refs_2_, ...), custom_call_target="tpu_custom_call" | custom-call | tf_op jit(solution)/shard_map/pallas_call | solution.py:289
  32.1 0.8 %shard_map.52 = (f32[128,256]{1,0:T(8,128)}, f32[1,128]{1,0:T(1,128)}) custom-call(f32[264,128]{1,0:T(8,128)S(1)} %shard_map.51.final), custom_call_target="tpu_custom_call" | custom-call | tf_op jit(solution)/shard_map/pallas_call | solution.py:299

commit v5 on v4

--- a/solution.py
+++ b/solution.py
@@ -148,15 +148,22 @@
             src_ref=src, dst_ref=dst, send_sem=s, recv_sem=t, device_id=dev, device_id_type=MESH
         )
 
+    half = blocks // 2
+
     def across(q, r):
         out, come, _, _, s, t, _, _ = buffers[q]
-        return rcopy(out.at[r], come.at[r], s.at[r], t.at[r], core)
-
-    def message(q, r, step):
+        return rcopy(out.at[r], come.at[r], s, t.at[r], core)
+
+    def message(q, r):
         _, _, acc, got, _, _, s, t = buffers[q]
+        step = depth - r.bit_length()
         (d0, r0), (d1, r1) = (order[step] for order in parts[q][2])
         peer = ((1 - c) * flip(me_d, d0) + c * flip(me_d, d1), (1 - c) * flip(me_r, r0) + c * flip(me_r, r1))
-        return rcopy(acc.at[r], got.at[r], s.at[r], t.at[r], peer)
+        return rcopy(acc.at[r], got.at[r], s, t.at[r - (half >> step)], peer)
+
+    def arrived(q, r, n):
+        _, _, acc, got, _, _, s, t = buffers[q]
+        rcopy(acc.at[pl.ds(0, n)], got.at[pl.ds(0, n)], s, t.at[r], core).wait_recv()
 
     bases = [4 * blocks * sum(p[1] for p in parts[:q]) for q in range(len(parts))]
 
@@ -170,14 +177,15 @@
         if q == 0:
             put(slice(words, words + 1), cnt_ref[pl.ds(other * blocks + r, 1), :])
 
-    def total(q, r, step, put):
+    def total(q, r, put):
         _, come, _, got = buffers[q][:4]
         across(q, r).wait_recv()
         come_from = [come.at[r]]
+        step = depth - r.bit_length()
+        if step:
+            arrived(q, r, step)
         for k in range(step):
-            at = r + (blocks >> (k + 1))
-            message(q, at, k).wait_recv()
-            come_from.append(got.at[at])
+            come_from.append(got.at[r + (half >> k)])
 
         def add(rows, v):
             for ref in come_from:
@@ -194,33 +202,24 @@
     pl.semaphore_wait(barrier, len(peers))
 
     def forward(q, r):
-        step = depth - r.bit_length()
-        total(q, r, step, into(buffers[q][2], r))
-        message(q, r, step).start()
+        total(q, r, into(buffers[q][2], r))
+        message(q, r).start()
 
     order = turns(blocks, parts)
-    lead = next(n for n, (q, r) in enumerate(order) if r < blocks // 2)
+    lead = next(n for n, (q, r) in enumerate(order) if r < half)
     for n, (q, r) in enumerate(order):
         local(q, 1, r, into(buffers[q][0], r))
         across(q, r).start()
         if LAG <= n < lead + LAG:
             forward(*order[n - LAG])
-    for q, r in order[lead:]:
+    for q, r in order[min(lead, len(order) - LAG):]:
         if r:
             forward(q, r)
-
-    @pl.loop(0, blocks)
-    def _(r):
-        for q in range(len(parts)):
-            across(q, r).wait_send()
-
-    for step in range(depth):
-        size = blocks >> (step + 1)
-
-        @pl.loop(size, 2 * size)
-        def _(r):
-            for q in range(len(parts)):
-                message(q, r, step).wait_send()
+    for q in range(len(parts)):
+        out, come, acc, got, s, t, s2, t2 = buffers[q]
+        rcopy(out, come, s, t.at[0], core).wait_send()
+        rest = pl.ds(1, blocks - 1)
+        rcopy(acc.at[rest], got.at[rest], s2, t2.at[0], core).wait_send()
 
     for q in reversed(range(len(parts))):
         first, keys, _ = parts[q]
@@ -231,7 +230,7 @@
             else:
                 final[2 * kpd:2 * kpd + 1, :] = v
 
-        total(q, 0, depth, put)
+        total(q, 0, put)
 
 
 def divide(kpd, final, out_hbm, cout_hbm, out_ref, cout_ref, osem):
@@ -261,7 +260,7 @@
         return pltpu.VMEM(shape, dtype)
 
     def dma(*shape):
-        return [pltpu.SemaphoreType.DMA(shape)] * 2 if shape else [pltpu.SemaphoreType.DMA] * 2
+        return pltpu.SemaphoreType.DMA(shape) if shape else pltpu.SemaphoreType.DMA
 
     I32 = jnp.int32
     pin = pltpu.with_memory_space_constraint
@@ -285,7 +284,8 @@
 
     scratch = []
     for q, (_, keys, _) in enumerate(parts):
-        scratch += [vm(blocks, 2 * keys + (q == 0), LANES)] * 4 + dma(blocks) + dma(blocks)
+        scratch += [vm(blocks, 2 * keys + (q == 0), LANES)] * 4
+        scratch += [dma(), dma(blocks), dma(), dma(blocks // 2)]
     final = pl.pallas_call(
         functools.partial(kernel, parts, n_dom, n_rep),
         out_shape=vm(2 * kpd + 8, LANES),

time: 33 us -> 32 us (0.970)
  Pallas kernels: 32.3 us -> 31.2 us
    pallas_call x1, Pallas kernels: 25.4 us -> 24.4 us  [per_device(): pl.pallas_call(functools.partial(kernel, parts, n_dom, n_rep), out_shape=...]
where the time goes in v5:
time: 32 us; the launch traced here: 31.9 us
  Pallas kernels  31.2 us (98%)
  between operations  0.65 us (2%)
    pallas_call x1, Pallas kernels, per_device(): pl.pallas_call(functools.partial(kernel, parts, n_dom, n_rep), out_shape=...  24.4 us
    pallas_call x1, Pallas kernels, per_device(): pl.pallas_call(functools.partial(scatter, parts, n_dom, n_rep, rows), out...  6.03 us
    pallas_call x1, Pallas kernels, per_device(): pl.pallas_call(functools.partial(divide, kpd), out_shape=(jax.ShapeDtypeS...  0.77 us

profile of v5, /device:TPU:0, one launch (start us, length us, event | category | flops | bytes accessed | tf_op | source)
XLA Modules:
  0.0 31.9 jit_solution(4833237684896339582)
XLA Ops:
  0.6 6.0 %shard_map.50 = (f32[8192,128]{1,0:T(8,128)S(1)}, f32[8192,128]{1,0:T(8,128)S(1)}, f32[8192,128]{1,0:T(8,128)S(1)}, f32[8192,128]{1,0:T(8,128)S(1)}, f32[8192,12...) custom-call(s32[32,128]{1,0:T(8,128)} %bitcast.11, ...), custom_call_target="tpu_custom_call" | custom-call | tf_op jit(solution)/shard_map/pallas_call | solution.py:272
  6.7 24.4 %shard_map.51.final = f32[264,128]{1,0:T(8,128)S(1)} custom-call(f32[32,128]{1,0:T(8,128)S(1)} %get-tuple-element.12.cnt_ref, f32[8192,128]{1,0:T(8,128)S(1)} %get-tuple-element.13.refs_0_, f32[8192,128]{1,0:T(8,128)S(1)} %get-tuple-element.14.refs_1_, f32[8192,128]{1,0:T(8,128)S(1)} %get-tuple-element.15.refs_2_, ...), custom_call_target="tpu_custom_call" | custom-call | tf_op jit(solution)/shard_map/pallas_call | solution.py:289
  31.1 0.8 %shard_map.52 = (f32[128,256]{1,0:T(8,128)}, f32[1,128]{1,0:T(1,128)}) custom-call(f32[264,128]{1,0:T(8,128)S(1)} %shard_map.51.final), custom_call_target="tpu_custom_call" | custom-call | tf_op jit(solution)/shard_map/pallas_call | solution.py:299

commit v6 on v5

--- a/solution.py
+++ b/solution.py
@@ -15,9 +15,10 @@
 TABLES = 7
 LAG = 8
 TURNS = (
-    31, 40, 15, 29, 30, 47, 45, 44, 27, 46, 23, 7, 41, 11, 39, 25,
-    13, 37, 14, 43, 19, 26, 21, 3, 22, 36, 9, 38, 5, 6, 28, 17,
-    42, 10, 12, 18, 24, 35, 8, 1, 20, 2, 34, 33, 4, 32, 16, 0,
+    31, 44, 46, 15, 63, 14, 27, 40, 60, 47, 29, 45, 43, 62, 59, 23,
+    36, 55, 13, 11, 57, 30, 25, 52, 58, 10, 7, 39, 61, 9, 21, 6,
+    12, 37, 26, 19, 56, 28, 5, 54, 53, 51, 8, 3, 22, 38, 42, 41,
+    17, 35, 2, 50, 1, 24, 4, 33, 49, 18, 34, 20, 48, 32, 16, 0,
 )
 
 
@@ -38,13 +39,13 @@
     x, y = (0, 1), (2, 0)
     rest = [(1 << b, 0) for b in range(2, log2(n_dom))] + [(0, 1 << b) for b in range(1, log2(n_rep))]
     flat, tall = ([x, y, *rest], [y, x, *rest]), ([*rest, y, x], [*rest, x, y])
-    cuts = [kpd * at // 128 // 4 * 4 for at in (0, 52, 100)] + [kpd]
-    ways = [flat, flat, tall]
+    cuts = [kpd * at // 128 // 4 * 4 for at in (0, 52, 100, 116)] + [kpd]
+    ways = [flat, flat, tall, tall]
     return [(cuts[q], cuts[q + 1] - cuts[q], way) for q, way in enumerate(ways) if cuts[q] < cuts[q + 1]]
 
 
 def turns(blocks, parts):
-    if blocks == 16 and len(parts) == 3:
+    if blocks == 16 and len(parts) == 4:
         return [divmod(turn, 16) for turn in TURNS]
     return [(q, r) for r in reversed(range(blocks)) for q in range(len(parts))]
 
@@ -152,7 +153,8 @@
 
     def across(q, r):
         out, come, _, _, s, t, _, _ = buffers[q]
-        return rcopy(out.at[r], come.at[r], s, t.at[r], core)
+        at, n = (r, r - half // 2) if r >= half else (pl.ds(r // 2 * 2, 2), r // 2)
+        return rcopy(out.at[at], come.at[at], s, t.at[n], core)
 
     def message(q, r):
         _, _, acc, got, _, _, s, t = buffers[q]
@@ -177,9 +179,13 @@
         if q == 0:
             put(slice(words, words + 1), cnt_ref[pl.ds(other * blocks + r, 1), :])
 
+    paired = set()
+
     def total(q, r, put):
         _, come, _, got = buffers[q][:4]
-        across(q, r).wait_recv()
+        if r >= half or (q, r // 2) not in paired:
+            across(q, r).wait_recv()
+            paired.add((q, r // 2))
         come_from = [come.at[r]]
         step = depth - r.bit_length()
         if step:
@@ -207,9 +213,14 @@
 
     order = turns(blocks, parts)
     lead = next(n for n, (q, r) in enumerate(order) if r < half)
+    sent = set()
     for n, (q, r) in enumerate(order):
-        local(q, 1, r, into(buffers[q][0], r))
-        across(q, r).start()
+        pair = [r] if r >= half else [r // 2 * 2, r // 2 * 2 + 1]
+        if (q, r) not in sent:
+            for k in pair:
+                local(q, 1, k, into(buffers[q][0], k))
+                sent.add((q, k))
+            across(q, r).start()
         if LAG <= n < lead + LAG:
             forward(*order[n - LAG])
     for q, r in order[min(lead, len(order) - LAG):]:
@@ -285,7 +296,7 @@
     scratch = []
     for q, (_, keys, _) in enumerate(parts):
         scratch += [vm(blocks, 2 * keys + (q == 0), LANES)] * 4
-        scratch += [dma(), dma(blocks), dma(), dma(blocks // 2)]
+        scratch += [dma(), dma(blocks // 2 + blocks // 4), dma(), dma(blocks // 2)]
     final = pl.pallas_call(
         functools.partial(kernel, parts, n_dom, n_rep),
         out_shape=vm(2 * kpd + 8, LANES),

time: 32 us -> 31.7 us (level)
    pallas_call x1, Pallas kernels: 24.4 us -> 24.1 us  [per_device(): pl.pallas_call(functools.partial(kernel, parts, n_dom, n_rep), out_shape=...]
where the time goes in v6:
time: 31.7 us; the launch traced here: 31.5 us
  Pallas kernels  30.9 us (97%)
  between operations  0.65 us (2%)
    pallas_call x1, Pallas kernels, per_device(): pl.pallas_call(functools.partial(kernel, parts, n_dom, n_rep), out_shape=...  24.1 us
    pallas_call x1, Pallas kernels, per_device(): pl.pallas_call(functools.partial(scatter, parts, n_dom, n_rep, rows), out...  6.04 us
    pallas_call x1, Pallas kernels, per_device(): pl.pallas_call(functools.partial(divide, kpd), out_shape=(jax.ShapeDtypeS...  0.77 us

profile of v6, /device:TPU:0, one launch (start us, length us, event | category | flops | bytes accessed | tf_op | source)
XLA Modules:
  0.0 31.5 jit_solution(17749838892432568234)
XLA Ops:
  0.6 6.0 %shard_map.50 = (f32[8192,128]{1,0:T(8,128)S(1)}, f32[8192,128]{1,0:T(8,128)S(1)}, f32[8192,128]{1,0:T(8,128)S(1)}, f32[8192,128]{1,0:T(8,128)S(1)}, f32[8192,12...) custom-call(s32[32,128]{1,0:T(8,128)} %bitcast.11, ...), custom_call_target="tpu_custom_call" | custom-call | tf_op jit(solution)/shard_map/pallas_call | solution.py:283
  6.7 24.1 %shard_map.51.final = f32[264,128]{1,0:T(8,128)S(1)} custom-call(f32[32,128]{1,0:T(8,128)S(1)} %get-tuple-element.12.cnt_ref, f32[8192,128]{1,0:T(8,128)S(1)} %get-tuple-element.13.refs_0_, f32[8192,128]{1,0:T(8,128)S(1)} %get-tuple-element.14.refs_1_, f32[8192,128]{1,0:T(8,128)S(1)} %get-tuple-element.15.refs_2_, ...), custom_call_target="tpu_custom_call" | custom-call | tf_op jit(solution)/shard_map/pallas_call | solution.py:300
  30.8 0.8 %shard_map.52 = (f32[128,256]{1,0:T(8,128)}, f32[1,128]{1,0:T(1,128)}) custom-call(f32[264,128]{1,0:T(8,128)S(1)} %shard_map.51.final), custom_call_target="tpu_custom_call" | custom-call | tf_op jit(solution)/shard_map/pallas_call | solution.py:310

commit v7 on v6

--- a/solution.py
+++ b/solution.py
@@ -151,8 +151,12 @@
 
     half = blocks // 2
 
+    def twins(q):
+        return range(q // 2 * 2, min(q // 2 * 2 + 2, len(parts)))
+
     def across(q, r):
-        out, come, _, _, s, t, _, _ = buffers[q]
+        out, come, _, _, s = buffers[q][:5]
+        t = buffers[q // 2 * 2][5]
         at, n = (r, r - half // 2) if r >= half else (pl.ds(r // 2 * 2, 2), r // 2)
         return rcopy(out.at[at], come.at[at], s, t.at[n], core)
 
@@ -183,9 +187,12 @@
 
     def total(q, r, put):
         _, come, _, got = buffers[q][:4]
-        if r >= half or (q, r // 2) not in paired:
-            across(q, r).wait_recv()
-            paired.add((q, r // 2))
+        n = r - half // 2 if r >= half else r // 2
+        if (q // 2, n) not in paired:
+            words = sum(2 * parts[k][1] + (k == 0) for k in twins(q)) * (1 if r >= half else 2)
+            some = tabs[0].at[pl.ds(0, words)]
+            rcopy(some, some, buffers[q][4], buffers[q // 2 * 2][5].at[n], core).wait_recv()
+            paired.add((q // 2, n))
         come_from = [come.at[r]]
         step = depth - r.bit_length()
         if step:
@@ -217,10 +224,11 @@
     for n, (q, r) in enumerate(order):
         pair = [r] if r >= half else [r // 2 * 2, r // 2 * 2 + 1]
         if (q, r) not in sent:
-            for k in pair:
-                local(q, 1, k, into(buffers[q][0], k))
-                sent.add((q, k))
-            across(q, r).start()
+            for j in twins(q):
+                for k in pair:
+                    local(j, 1, k, into(buffers[j][0], k))
+                    sent.add((j, k))
+                across(j, r).start()
         if LAG <= n < lead + LAG:
             forward(*order[n - LAG])
     for q, r in order[min(lead, len(order) - LAG):]:
@@ -228,7 +236,7 @@
             forward(q, r)
     for q in range(len(parts)):
         out, come, acc, got, s, t, s2, t2 = buffers[q]
-        rcopy(out, come, s, t.at[0], core).wait_send()
+        rcopy(out, come, s, t2.at[0], core).wait_send()
         rest = pl.ds(1, blocks - 1)
         rcopy(acc.at[rest], got.at[rest], s2, t2.at[0], core).wait_send()
 
@@ -296,7 +304,7 @@
     scratch = []
     for q, (_, keys, _) in enumerate(parts):
         scratch += [vm(blocks, 2 * keys + (q == 0), LANES)] * 4
-        scratch += [dma(), dma(blocks // 2 + blocks // 4), dma(), dma(blocks // 2)]
+        scratch += [dma(), dma(blocks // 2 + blocks // 4) if q % 2 == 0 else dma(), dma(), dma(blocks // 2)]
     final = pl.pallas_call(
         functools.partial(kernel, parts, n_dom, n_rep),
         out_shape=vm(2 * kpd + 8, LANES),

time: 31.7 us -> 31.6 us (level)
  no operation moved by 1% of the time
where the time goes in v7:
time: 31.6 us; the launch traced here: 31.4 us
  Pallas kernels  30.8 us (97%)
  between operations  0.65 us (2%)
    pallas_call x1, Pallas kernels, per_device(): pl.pallas_call(functools.partial(kernel, parts, n_dom, n_rep), out_shape=...  24 us
    pallas_call x1, Pallas kernels, per_device(): pl.pallas_call(functools.partial(scatter, parts, n_dom, n_rep, rows), out...  6.04 us
    pallas_call x1, Pallas kernels, per_device(): pl.pallas_call(functools.partial(divide, kpd), out_shape=(jax.ShapeDtypeS...  0.77 us

profile of v7, /device:TPU:0, one launch (start us, length us, event | category | flops | bytes accessed | tf_op | source)
XLA Modules:
  0.0 31.4 jit_solution(17243763107252678824)
XLA Ops:
  0.6 6.0 %shard_map.50 = (f32[8192,128]{1,0:T(8,128)S(1)}, f32[8192,128]{1,0:T(8,128)S(1)}, f32[8192,128]{1,0:T(8,128)S(1)}, f32[8192,128]{1,0:T(8,128)S(1)}, f32[8192,12...) custom-call(s32[32,128]{1,0:T(8,128)} %bitcast.11, ...), custom_call_target="tpu_custom_call" | custom-call | tf_op jit(solution)/shard_map/pallas_call | solution.py:291
  6.7 24.0 %shard_map.51.final = f32[264,128]{1,0:T(8,128)S(1)} custom-call(f32[32,128]{1,0:T(8,128)S(1)} %get-tuple-element.12.cnt_ref, f32[8192,128]{1,0:T(8,128)S(1)} %get-tuple-element.13.refs_0_, f32[8192,128]{1,0:T(8,128)S(1)} %get-tuple-element.14.refs_1_, f32[8192,128]{1,0:T(8,128)S(1)} %get-tuple-element.15.refs_2_, ...), custom_call_target="tpu_custom_call" | custom-call | tf_op jit(solution)/shard_map/pallas_call | solution.py:308
  30.6 0.8 %shard_map.52 = (f32[128,256]{1,0:T(8,128)}, f32[1,128]{1,0:T(1,128)}) custom-call(f32[264,128]{1,0:T(8,128)S(1)} %shard_map.51.final), custom_call_target="tpu_custom_call" | custom-call | tf_op jit(solution)/shard_map/pallas_call | solution.py:318
